TPU v7x, 32 devices: a whole 2x2x4 slice. The times are simulated.
32 devices in a mesh: scen: 8 (over z, x), rootr: 2 (over core), rootc: 2 (over y).
Axes of the slice: x: 2, y: 2, z: 4, core: 2. Of those that a mesh axis runs over, the one named last changes fastest.
Arguments:
- start_guess: float32 [8192, 256], P(('scen', 'rootr'), 'rootc'), may hold values from -6 to 6
- right_side: float32 [8192, 256], P(('scen', 'rootr'), 'rootc'), may hold values from -6 to 6
- root_diagonal: float32 [8192], P(('scen', 'rootr')), may hold values from 1 to 4
- preconditioner: bfloat16 [8192, 8192], P(('scen', 'rootr')), may hold values from -0.015625 to 0.015625
- border_block: bfloat16 [16, 512, 768], P(('scen', 'rootr'), 'rootc'), may hold values from -0.21875 to 0.21875
- coupling_inverse: bfloat16 [16, 512, 512], P(('scen', 'rootr'), 'rootc'), may hold values from -0.25 to 0.25
- border_count: int32 [16], P(('scen', 'rootr')), may hold values from 64 to 512, as said below
- column_tiles: int32 [16, 6], P(('scen', 'rootr')), may hold values from 0 to 63, as said below
Outputs:
- final_iterate: float32 [8192, 256], P(('scen', 'rootr'), 'rootc')
Inputs may be any that keep to these rules, and one draw needn't show every extreme that they name: A scenario's live border rows are its first border_count rows; some scenario has exactly 512. `column_tiles`: each row names 6 different tiles in rising order.
All inputs are finite; a program needn't handle non-finite values.
Results may differ from a plain program's by a relative error of at most 0.0022.
Values may be sent and summed in bfloat16 or wider, within the bound.
A program may use at most 64 MiB of HBM per device.

v0:
```python
import jax
import jax.numpy as jnp
from jax import lax
from jax.sharding import PartitionSpec as P

TILE = 128


def border_product(matrix, operand, live_here):
    half_rows = matrix.shape[0]
    live_mask = (jnp.arange(half_rows) < live_here)[:, None]
    product = jnp.dot(matrix, operand, preferred_element_type=jnp.float32)
    return jnp.where(live_mask, product, 0.0).astype(jnp.bfloat16)


def border_transpose(border, solved):
    numbers = (((0,), (0,)), ((), ()))
    return lax.dot_general(border, solved, numbers, preferred_element_type=jnp.float32)


def local(
    start_guess,
    right_side,
    root_diagonal,
    preconditioner,
    border_block,
    coupling_inverse,
    border_count,
    column_tiles,
):
    own_rows = start_guess.shape[0]
    half_rhs = start_guess.shape[1]
    half_rows = border_block.shape[1]
    coupled_cols = border_block.shape[2]
    order_rows = preconditioner.shape[1]
    border = border_block[0]
    inverse_rows = coupling_inverse[0]
    tile_ids = column_tiles[0]
    offset = lax.axis_index("rootc") * half_rows
    live_here = jnp.clip(border_count[0] - offset, 0, half_rows)
    iterate = start_guess
    own_low = iterate.astype(jnp.bfloat16)
    both_halves = lax.all_gather(own_low, "rootc", axis=1, tiled=True)
    gathered = lax.all_gather(both_halves, ("scen", "rootr"), axis=0, tiled=True)
    all_rhs = gathered.shape[1]
    picked = gathered.reshape(order_rows // TILE, TILE, all_rhs)[tile_ids].reshape(
        coupled_cols, all_rhs
    )
    values_local = border_product(border, picked, live_here)
    values_whole = lax.all_gather(values_local, "rootc", axis=0, tiled=True)
    solved = border_product(inverse_rows, values_whole, live_here)
    term_part = border_transpose(border, solved)
    term_half = lax.psum_scatter(term_part, "rootc", scatter_dimension=1, tiled=True)
    spread_terms = jnp.zeros((order_rows // TILE, TILE, half_rhs), jnp.float32)
    spread_terms = (
        spread_terms.at[tile_ids]
        .add(term_half.reshape(-1, TILE, half_rhs))
        .reshape(order_rows, half_rhs)
    )
    own_terms = right_side - root_diagonal[:, None] * iterate
    first_row = lax.axis_index(("scen", "rootr")) * own_rows
    current = lax.dynamic_slice_in_dim(spread_terms, first_row, own_rows, 0)
    spread_terms = lax.dynamic_update_slice_in_dim(spread_terms, current + own_terms, first_row, 0)
    residual = lax.psum(spread_terms, ("scen", "rootr"))
    update = jnp.dot(
        preconditioner, residual.astype(jnp.bfloat16), preferred_element_type=jnp.float32
    )
    iterate = iterate + update
    return iterate


def solution(mesh):
    placed = (
        P(("scen", "rootr"), "rootc"),
        P(("scen", "rootr"), "rootc"),
        P(("scen", "rootr")),
        P(("scen", "rootr"), None),
        P(("scen", "rootr"), "rootc", None),
        P(("scen", "rootr"), "rootc", None),
        P(("scen", "rootr")),
        P(("scen", "rootr"), None),
    )
    return jax.shard_map(
        local, mesh=mesh, in_specs=placed, out_specs=P(("scen", "rootr"), "rootc"), check_vma=False
    )
```

profile of v0, /device:TPU:0, one launch (start us, length us, event | category | flops | bytes accessed | tf_op | source)
XLA Modules:
  0.0 211.8 jit_solution(9271630107999515381)
XLA Ops:
  6.5 0.0 copy-start
  6.5 0.0 all-gather.2.cloned.1.call-start
  6.5 1.0 convert_element_type.16
  7.6 7.3 %all_gather.9 = bf16[512,256]{1,0:T(8,128)(2,1)} all-gather(bf16[512,128]{1,0:T(8,128)(2,1)S(1)} %convert_element_type.16), channel_id=1, replica_groups=mesh['scen'=8,'rootr'=2,'rootc'=2] {'rootc'}, dimensions={1}, use_global_device_ids=true | all-gather | bytes 393216 | tf_op jit(solution)/shard_map/all_gather | solution.py:43
  14.9 0.0 all-gather.2.cloned.1.call-update
  14.9 0.0 reduce-scatter.2.cloned.1.call-start
  15.6 0.7 fusion.17
  16.3 50.6 %all-gather.2.cloned.1.call-done = bf16[8192,256]{1,0:T(8,128)(2,1)} async-done(((bf16[512,256]{1,0:T(8,128)(2,1)}), bf16[8192,256]{1,0:T(8,128)(2,1)}) %all-gather.2.cloned.1.call-update) | async-done | bytes 4194320 | tf_op jit(solution)/shard_map/all_gather | solution.py:44
  66.9 2.8 %gather_fusion = bf16[6,128,256]{2,1,0:T(8,128)(2,1)S(1)} fusion(bf16[64,128,256]{2,1,0:T(8,128)(2,1)} %bitcast.34, s32[1024]{0:T(1024)S(1)} %pad_clamp_fusion), kind=kCustom, calls=%fused_computation | custom fusion | bytes 786456 | tf_op jit(solution)/shard_map/gather | solution.py:46
  69.7 0.0 copy-done
  69.7 0.3 fusion.10
  70.0 6.3 %all_gather.11 = bf16[512,256]{0,1:T(8,128)(2,1)S(1)} all-gather(bf16[256,256]{0,1:T(8,128)(2,1)S(1)} %fusion.10), channel_id=1, replica_groups=mesh['scen'=8,'rootr'=2,'rootc'=2] {'rootc'}, dimensions={0}, use_global_device_ids=true | all-gather | bytes 393216 | tf_op jit(solution)/shard_map/all_gather | solution.py:50
  76.3 2.4 %convolution_bitcast_fusion = f32[768,256]{0,1:T(8,128)} fusion(bf16[512,256]{0,1:T(8,128)(2,1)S(1)} %all_gather.11, bf16[1,256,768]{2,1,0:T(8,128)(2,1)S(1)} %copy-done, bf16[1,256,512]{2,1,0:T(8,128)(2,1)} %param.13, pred[256]{0:T(512)(128)(4,1)S(1)} %iota_compare_fusion), kind=kOutput, calls=%fused_computation.4 | convolution fusion | flops 167903232 | bytes 1704192 | tf_op jit(solution)/shard_map/dot_general | solution.py:18
  78.8 0.0 reduce-scatter.2.cloned.1.call-update
  78.8 0.1 copy.12
  78.9 16.1 %reduce-scatter.2.cloned.1.call-done = f32[768,128]{0,1:T(8,128)} async-done(((f32[768,256]{0,1:T(8,128)}), f32[768,128]{0,1:T(8,128)}) %reduce-scatter.2.cloned.1.call-update) | async-done | bytes 393232 | tf_op jit(solution)/shard_map/reduce_scatter | solution.py:53
  95.0 1.1 copy.11
  96.2 2.5 %broadcast_in_dim.24 = f32[64,128,128]{2,1,0:T(8,128)} broadcast(f32[]{:T(128)} %constant.10.clone.1), dimensions={} | broadcast | bytes 4194308 | tf_op jit(solution)/shard_map/broadcast_in_dim | solution.py:54
  98.6 2.6 %scatter_fusion = f32[64,128,128]{2,1,0:T(8,128)} fusion(f32[64,128,128]{2,1,0:T(8,128)} %broadcast_in_dim.24, s32[6]{0:T(128)S(1)} %fusion.17, f32[6,128,128]{2,1,0:T(8,128)S(1)} %bitcast.32), kind=kCustom, calls=%fused_computation.1 | custom fusion | flops 98304 | bytes 1179672 | tf_op jit(solution)/shard_map/scatter-add | solution.py:57
  101.2 0.0 copy-done.3
  101.2 1.8 add_dynamic-update-slice_fusion
  103.0 94.9 %all-reduce.1 = bf16[8192,128]{1,0:T(8,128)(2,1)S(1)} all-reduce(f32[8192,128]{1,0:T(8,128)} %add_dynamic-update-slice_fusion), channel_id=1, replica_groups=mesh['scen'=8,'rootr'=2,'rootc'=2] {'scen','rootr'}, use_global_device_ids=true, to_apply=%region_2.3 | all-reduce | flops 1048576 | bytes 6291456 | tf_op jit(solution)/shard_map/psum | solution.py:64
  197.9 6.3 %fusion.5 = f32[512,128]{0,1:T(8,128)S(1)} fusion(f32[512,128]{0,1:T(8,128)S(1)} %copy.12, bf16[512,8192]{1,0:T(8,128)(2,1)} %param.11, bf16[8192,128]{1,0:T(8,128)(2,1)S(1)} %all-reduce.1), kind=kOutput, calls=%fused_computation.8 | convolution fusion | flops 1073807360 | bytes 11010048 | tf_op jit(solution)/shard_map/dot_general | solution.py:65
  204.2 0.8 copy.13
  (7 shorter events, 0.0 us)
Async XLA Ops:
  6.5 63.1 %copy-start = (bf16[1,256,768]{2,1,0:T(8,128)(2,1)S(1)}, bf16[1,256,768]{2,1,0:T(8,128)(2,1)}, u32[]{:S(2)}) copy-start(bf16[1,256,768]{2,1,0:T(8,128)(2,1)} %param.12) | copy-start | bytes 1179652
  6.5 72.3 %copy-start.1 = (f32[512,128]{1,0:T(8,128)S(1)}, f32[512,128]{1,0:T(8,128)}, u32[]{:S(2)}) copy-start(f32[512,128]{1,0:T(8,128)} %param.8) | copy-start | bytes 786436
  6.5 60.4 %all-gather.2.cloned.1.call-start = ((), (), s32[]{:S(2)}) async-start(), calls=%async_computation.1 | async-start | bytes 4456448 | tf_op jit(solution)/shard_map/all_gather | solution.py:44
  14.9 80.1 %reduce-scatter.2.cloned.1.call-start = ((), (), s32[]{:S(2)}) async-start(), calls=%async_computation.2 | async-start | bytes 1179648 | tf_op jit(solution)/shard_map/reduce_scatter | solution.py:53
  76.3 24.9 %copy-start.2 = (f32[512,128]{1,0:T(8,128)S(1)}, f32[512,128]{1,0:T(8,128)}, u32[]{:S(2)}) copy-start(f32[512,128]{1,0:T(8,128)} %param.9) | copy-start | bytes 786436
  76.3 24.9 %copy-start.3 = (f32[512]{0:T(512)S(1)}, f32[512]{0:T(512)}, u32[]{:S(2)}) copy-start(f32[512]{0:T(512)} %param.10) | copy-start | bytes 6148
Sparse Core Ops, SparseCore 0:
  15.0 51.8 all-gather.1
  78.9 16.0 reduce-scatter.1
where the time goes:
time: 213 us; the launch traced here: 212 us
  blocking collectives  108 us (51%)
  waiting for transfers between devices  66.7 us (31%)
  between operations  14.1 us (7%)
  matrix products  9.03 us (4%)
  local copies, waits for them, and re-layouts  7.34 us (3%)
  other arithmetic  6.05 us (3%)
    psum x1, blocking collectives, local(): residual = lax.psum(spread_terms, ('scen', 'rootr'))  94.9 us
    all_gather x1, waiting for transfers between devices, local(): lax.all_gather(both_halves, ('scen', 'rootr'), axis=0, tiled=True)  50.6 us
    reduce_scatter x1, waiting for transfers between devices, local(): lax.psum_scatter(term_part, 'rootc', scatter_dimension=1, tiled=True)  16.1 us
    all_gather x1, blocking collectives, local(): both_halves = lax.all_gather(own_low, 'rootc', axis=1, tiled=True)  7.29 us
    all_gather x1, blocking collectives, local(): values_whole = lax.all_gather(values_local, 'rootc', axis=0, tiled=True)  6.31 us
    dot_general x1, matrix products, local(): jnp.dot(preconditioner, residual.astype(jnp.bfloat16), preferred_element_...  6.28 us
  transfers between devices with their start and end apart: 2, of which 2 were waited for; matrix products, arithmetic and copies ran while one was open for 0% of the time, Pallas kernels for 0%

commit v1 on v0

v1 whole, which is shorter than its diff:
```python
import functools
import math

import jax
import jax.numpy as jnp
from jax import lax
from jax.experimental import pallas as pl
from jax.experimental.pallas import tpu as pltpu
from jax.sharding import PartitionSpec as P

TILE = 128
CHUNKS = 2
MESH = pl.DeviceIdType.MESH


class Gather:
    def __init__(self, place, buf, rows, sems):
        chunks = min(CHUNKS, rows)
        self.place, self.buf, self.chunks = place, buf, chunks
        self.step = rows // chunks
        self.rows = rows
        self.ring_send, self.ring_recv, self.pair_send, self.pair_recv = sems
        self.sent = []

    def piece(self, scen, core, chunk):
        first = (scen * 2 + core) * self.rows + chunk * self.step
        return self.buf.at[pl.ds(first, self.step)]

    def slot(self, way, hop, chunk):
        return (way * (self.place.hops + 1) + hop) * self.chunks + chunk

    def carried(self, way, hop):
        if hop < self.place.hops:
            return range(self.chunks)
        return [way] if way < self.chunks else []

    def ring_copy(self, way, hop, chunk, scen):
        at = self.slot(way, hop, chunk)
        ref = self.piece(scen, self.place.core, chunk)
        return pltpu.make_async_remote_copy(
            src_ref=ref,
            dst_ref=ref,
            send_sem=self.ring_send.at[at],
            recv_sem=self.ring_recv.at[at],
            device_id={"scen": self.place.ahead[way]},
            device_id_type=MESH,
        )

    def pair_copy(self, way, hop, chunk, scen, core):
        at = self.slot(way, hop, chunk)
        ref = self.piece(scen, core, chunk)
        return pltpu.make_async_remote_copy(
            src_ref=ref,
            dst_ref=ref,
            send_sem=self.pair_send.at[at],
            recv_sem=self.pair_recv.at[at],
            device_id={"rootr": 1 - self.place.core},
            device_id_type=MESH,
        )

    def send(self, copy):
        copy.start()
        self.sent.append(copy)

    def begin(self):
        for chunk in range(self.chunks):
            for way in range(2):
                if chunk in self.carried(way, 1):
                    self.send(self.ring_copy(way, 1, chunk, self.place.scen))
        for chunk in range(self.chunks):
            self.send(self.pair_copy(0, 0, chunk, self.place.scen, self.place.core))

    def advance(self, hop):
        for chunk in range(self.chunks):
            for way in range(2):
                if chunk not in self.carried(way, hop):
                    continue
                scen = self.place.origin(way, hop)
                self.ring_copy(way, hop, chunk, scen).wait_recv()
                if hop < self.place.hops and chunk in self.carried(way, hop + 1):
                    self.send(self.ring_copy(way, hop + 1, chunk, scen))
                self.send(self.pair_copy(way, hop, chunk, scen, self.place.core))

    def settle(self, hop):
        for chunk in range(self.chunks):
            for way in range(2):
                if hop == 0:
                    if way == 0:
                        self.pair_copy(0, 0, chunk, self.place.scen, 1 - self.place.core).wait_recv()
                elif chunk in self.carried(way, hop):
                    scen = self.place.origin(way, hop)
                    self.pair_copy(way, hop, chunk, scen, 1 - self.place.core).wait_recv()

    def finish(self):
        for copy in self.sent:
            copy.wait_send()


class Place:
    def __init__(self, count):
        self.count, self.hops = count, count // 2
        self.scen, self.core = lax.axis_index("scen"), lax.axis_index("rootr")
        side, level = lax.rem(self.scen, 2), lax.div(self.scen, 2)
        self.spot = level * (1 - side) + (count - 1 - level) * side
        self.ahead = [self.at(1), self.at(count - 1)]

    def at(self, shift):
        spot = lax.rem(self.spot + shift, self.count)
        upper = lax.div(spot, self.hops)
        return (1 - upper) * 2 * spot + upper * (2 * (self.count - 1 - spot) + 1)

    def origin(self, way, hop):
        return self.at(self.count - hop if way == 0 else hop)

    def origin_traced(self, way, hop):
        return self.at(self.count - hop + way * (2 * hop - self.count))


def kernel(
    count,
    guess_ref,
    right_ref,
    diagonal_ref,
    precon_hbm,
    border_hbm,
    inverse_hbm,
    live_ref,
    own_tiles_ref,
    tiles_row_ref,
    out_ref,
    low_all,
    own_all,
    term_all,
    tiles_all,
    tiles_smem,
    precon,
    border,
    inverse,
    local_sems,
    precon_sems,
    cross_send,
    cross_recv,
    *ring_sems,
):
    place = Place(count)
    side = lax.axis_index("rootc")
    own_rows, half_rhs = guess_ref.shape
    half_rows, coupled = border_hbm.shape[1:]
    touched = coupled // TILE
    own_block = place.scen * 2 + place.core

    own_half = pl.ds(pl.multiple_of(side * half_rows, half_rows), half_rows)
    other_half = pl.ds(pl.multiple_of((1 - side) * half_rows, half_rows), half_rows)
    load_border = pltpu.make_async_copy(border_hbm.at[0], border.at[own_half], local_sems.at[0])
    load_inverse = pltpu.make_async_copy(inverse_hbm.at[0], inverse.at[own_half], local_sems.at[1])
    columns_count = precon.shape[0]

    def load_column(t):
        columns = pl.ds(pl.multiple_of(t * TILE, TILE), TILE)
        return pltpu.make_async_copy(precon_hbm.at[:, columns], precon.at[t], precon_sems.at[t])

    load_border.start()
    load_inverse.start()

    unit = low_all.shape[1]
    units = own_rows // unit
    per_tile = TILE // unit
    own_slice = pl.ds(own_block * units, units)
    split = (units, unit, half_rhs)
    low_all[own_slice] = guess_ref[...].astype(jnp.bfloat16).reshape(split)
    scale = jnp.broadcast_to(diagonal_ref[...], (half_rhs, own_rows)).T
    own_terms = right_ref[...] - scale * guess_ref[...]
    own_all[own_slice] = own_terms.astype(jnp.bfloat16).reshape(split)
    tiles_all[pl.ds(own_block, 1)] = tiles_row_ref[...]

    barrier = pltpu.get_barrier_semaphore()
    for peer in (
        {"scen": place.ahead[0]},
        {"scen": place.ahead[1]},
        {"rootr": 1 - place.core},
        {"rootc": 1 - side},
    ):
        pl.semaphore_signal(barrier, inc=1, device_id=peer, device_id_type=MESH)
    pl.semaphore_wait(barrier, 4)

    low = Gather(place, low_all, units, ring_sems[0:4])
    own = Gather(place, own_all, units, ring_sems[4:8])
    term = Gather(place, term_all, touched, ring_sems[8:12])
    tiles = Gather(place, tiles_all, 1, ring_sems[12:16])

    crossings = []
    low.begin()
    for index, (source, target) in enumerate(((border_hbm, border), (inverse_hbm, inverse))):
        crossing = pltpu.make_async_remote_copy(
            src_ref=source.at[0],
            dst_ref=target.at[own_half],
            send_sem=cross_send.at[index],
            recv_sem=cross_recv.at[index],
            device_id={"rootc": 1 - side},
            device_id_type=MESH,
        )
        crossing.start()
        crossings.append(crossing)
    tiles.begin()

    @pl.loop(0, columns_count)
    def start_column(t):
        load_column(t).start()

    for hop in range(1, place.hops + 1):
        low.advance(hop)
        tiles.advance(hop)
    own.begin()
    for hop in range(place.hops + 1):
        low.settle(hop)

    load_border.wait()
    crossings[0].wait_recv()
    live = jnp.clip(live_ref[0], 0, 2 * half_rows)
    live_mask = lax.broadcasted_iota(jnp.int32, (2 * half_rows, half_rhs), 0) < live
    picked = jnp.concatenate(
        [
            low_all[own_tiles_ref[0, k] * per_tile + part]
            for k in range(touched)
            for part in range(per_tile)
        ],
        axis=0,
    )
    values = jnp.dot(border[...], picked, preferred_element_type=jnp.float32)
    values = jnp.where(live_mask, values, 0.0).astype(jnp.bfloat16)
    load_inverse.wait()
    crossings[1].wait_recv()
    solved = jnp.dot(inverse[...], values, preferred_element_type=jnp.float32)
    solved = jnp.where(live_mask, solved, 0.0).astype(jnp.bfloat16)
    terms = lax.dot_general(
        border[...], solved, (((0,), (0,)), ((), ())), preferred_element_type=jnp.float32
    )
    term_all[pl.ds(own_block * touched, touched)] = terms.astype(jnp.bfloat16).reshape(
        touched, TILE, half_rhs
    )
    term.begin()

    for hop in range(place.hops + 1):
        tiles.settle(hop)
    to_smem = pltpu.make_async_copy(tiles_all, tiles_smem, local_sems.at[3])
    to_smem.start()
    to_smem.wait()

    @pl.loop(0, columns_count)
    def wait_column(t):
        load_column(t).wait()

    out_ref[...] = guess_ref[...]

    def product(columns, values, rows):
        left = jnp.concatenate([precon[t] for t in columns], axis=1)
        right = jnp.concatenate([values[t] for t in rows], axis=0)
        return jnp.dot(left, right, preferred_element_type=jnp.float32)

    def add_block(index, hop):
        way, core = lax.div(index, 2), lax.rem(index, 2)
        block = place.origin_traced(way, hop) * 2 + core
        total = jnp.zeros_like(out_ref)
        if own_rows % TILE == 0:
            own_tiles = own_rows // TILE
            for k in range(0, own_tiles, 2):
                group = [block * own_tiles + j for j in range(k, min(k + 2, own_tiles))]
                total = total + product(group, own_all, group)
        for k in range(0, touched, 2):
            group = range(k, min(k + 2, touched))
            total = total + product(
                [tiles_smem[block, 0, j] for j in group],
                term_all,
                [block * touched + j for j in group],
            )
        out_ref[...] += total

    def absorb(hop):
        own.settle(hop)
        term.settle(hop)
        ways = 1 if hop in (0, place.hops) else 2

        def body(index, carry):
            add_block(index, hop)
            return carry

        lax.fori_loop(0, 2 * ways, body, 0)

    for hop in range(1, place.hops + 1):
        own.advance(hop)
        term.advance(hop)
        absorb(hop - 1)
    absorb(place.hops)
    if own_rows % TILE != 0:

        @pl.loop(0, columns_count)
        def add_own(t):
            rows = [t * per_tile + part for part in range(per_tile)]
            out_ref[...] += product([t], own_all, rows)

    for gather in (low, own, term, tiles):
        gather.finish()
    for crossing in crossings:
        crossing.wait_send()


def local(
    count,
    start_guess,
    right_side,
    root_diagonal,
    preconditioner,
    border_block,
    coupling_inverse,
    border_count,
    column_tiles,
):
    own_rows, half_rhs = start_guess.shape
    order = preconditioner.shape[1]
    half_rows, coupled = border_block.shape[1:]
    blocks = count * 2
    touched = column_tiles.shape[1]
    tiles_row = jnp.pad(column_tiles, ((0, 0), (0, 128 - touched)))[:, None, :]
    hops = count // 2
    ring_sems = []
    unit = math.gcd(own_rows, TILE)
    units = own_rows // unit
    for rows in (units, units, touched, 1):
        chunks = min(CHUNKS, rows)
        ring_sems += [pltpu.SemaphoreType.DMA((2 * (hops + 1) * chunks,))] * 4
    vmem = pl.BlockSpec(memory_space=pltpu.VMEM)
    smem = pl.BlockSpec(memory_space=pltpu.SMEM)
    anywhere = pl.BlockSpec(memory_space=pltpu.HBM)
    return pl.pallas_call(
        functools.partial(kernel, count),
        out_shape=jax.ShapeDtypeStruct((own_rows, half_rhs), jnp.float32),
        in_specs=[vmem, vmem, vmem, anywhere, anywhere, anywhere, smem, smem, vmem],
        out_specs=vmem,
        scratch_shapes=[
            pltpu.VMEM((order // unit, unit, half_rhs), jnp.bfloat16),
            pltpu.VMEM((order // unit, unit, half_rhs), jnp.bfloat16),
            pltpu.VMEM((blocks * touched, TILE, half_rhs), jnp.bfloat16),
            pltpu.VMEM((blocks, 1, 128), jnp.int32),
            pltpu.SMEM((blocks, 1, 128), jnp.int32),
            pltpu.VMEM((order // TILE, own_rows, TILE), jnp.bfloat16),
            pltpu.VMEM((2 * half_rows, coupled), jnp.bfloat16),
            pltpu.VMEM((2 * half_rows, 2 * half_rows), jnp.bfloat16),
            pltpu.SemaphoreType.DMA((4,)),
            pltpu.SemaphoreType.DMA((order // TILE,)),
            pltpu.SemaphoreType.DMA((2,)),
            pltpu.SemaphoreType.DMA((2,)),
        ]
        + ring_sems,
        compiler_params=pltpu.CompilerParams(
            collective_id=0, has_side_effects=True, vmem_limit_bytes=60 * 1024 * 1024
        ),
    )(
        start_guess,
        right_side,
        root_diagonal[None, :],
        preconditioner,
        border_block,
        coupling_inverse,
        border_count,
        column_tiles,
        tiles_row,
    )


def solution(mesh):
    rows = ("scen", "rootr")
    placed = (
        P(rows, "rootc"),
        P(rows, "rootc"),
        P(rows),
        P(rows, None),
        P(rows, "rootc", None),
        P(rows, "rootc", None),
        P(rows),
        P(rows, None),
    )
    return jax.shard_map(
        functools.partial(local, mesh.shape["scen"]),
        mesh=mesh,
        in_specs=placed,
        out_specs=P(rows, "rootc"),
        check_vma=False,
    )
```

time: 213 us -> 59.2 us (0.28)
  blocking collectives: 108 us -> 0 us
  waiting for transfers between devices: 66.7 us -> 0 us
  Pallas kernels: 0 us -> 55.5 us
  between operations: 14.1 us -> 0.66 us
  matrix products: 9.03 us -> 0 us
  other arithmetic: 6.05 us -> 0 us
  local copies, waits for them, and re-layouts: 7.34 us -> 2.84 us
    psum x1 -> x0, blocking collectives: 94.9 us -> none  [local(): residual = lax.psum(spread_terms, ('scen', 'rootr'))]
    pallas_call x0 -> x1, Pallas kernels: none -> 55.5 us  [local(): pl.pallas_call(functools.partial(kernel, count), out_shape=jax.ShapeDtype...]
    all_gather x1 -> x0, waiting for transfers between devices: 50.6 us -> none  [local(): lax.all_gather(both_halves, ('scen', 'rootr'), axis=0, tiled=True)]
    reduce_scatter x1 -> x0, waiting for transfers between devices: 16.1 us -> none  [local(): lax.psum_scatter(term_part, 'rootc', scatter_dimension=1, tiled=True)]
    all_gather x2 -> x0, blocking collectives: 13.6 us -> none  [the longest x1 7.29 us: local(): both_halves = lax.all_gather(own_low, 'rootc', axis=1, tiled=True)]
    dot_general x3 -> x0, matrix products: 9.03 us -> none  [the longest x1 6.28 us: local(): jnp.dot(preconditioner, residual.astype(jnp.bfloat16), preferred_element_...]
    gather x1 -> x0, local copies, waits for them, and re-layouts: 2.76 us -> none  [local(): gathered.reshape(order_rows // TILE, TILE, all_rhs)[tile_ids]]
    scatter-add x1 -> x0, other arithmetic: 2.57 us -> none  [local(): spread_terms = spread_terms.at[tile_ids].add(term_half.reshape(-1, TILE,...]
  transfers between devices with their start and end apart: 2 -> 0, of which waited for: 2 -> 0; matrix products, arithmetic and copies ran while one was open for 0% -> 0% of each run, Pallas kernels for 0% -> 0%
where the time goes in v1:
time: 59.2 us; the launch traced here: 59 us
  Pallas kernels  55.5 us (94%)
  local copies, waits for them, and re-layouts  2.84 us (5%)
  between operations  0.66 us (1%)
    pallas_call x1, Pallas kernels, local(): pl.pallas_call(functools.partial(kernel, count), out_shape=jax.ShapeDtype...  55.5 us
    unnamed x1, local copies, waits for them, and re-layouts  1.67 us

profile of v1, /device:TPU:0, one launch (start us, length us, event | category | flops | bytes accessed | tf_op | source)
XLA Modules:
  0.0 59.0 jit_solution(8244544112330665478)
XLA Ops:
  0.7 1.2 %pad_bitcast_fusion.tiles_row_ref = s32[1,1,128]{2,1,0:T(1,128)} fusion(s32[1,6]{1,0:T(1,128)} %own_tiles_ref.1), kind=kLoop, calls=%fused_computation | loop fusion | bytes 536 | tf_op jit(solution)/shard_map/broadcast_in_dim | solution.py:323
  1.8 55.5 %shard_map.82 = f32[512,128]{1,0:T(8,128)} custom-call(f32[512,128]{1,0:T(8,128)} %guess_ref.1, f32[512,128]{1,0:T(8,128)} %right_ref.1, f32[1,512]{1,0:T(1,128)} %bitcast.3, bf16[512,8192]{1,0:T(8,128)(2,1)} %precon_hbm.1, bf16[1,256,768]{2,1,0:T(8,128)(2,1)} %border_hbm.1, bf16[1,256,512]{2,1,0:T(8,128)(2,1)} %inverse_hbm.1, s32[1]{0:T(128)S(6)} %copy.10.live_ref, ...), custom_call_target="tpu_custom_call" | custom-call | tf_op jit(solution)/shard_map/pallas_call | solution.py:334
  57.3 1.7 %copy.11 = f32[512,128]{1,0:T(8,128)} copy(f32[512,128]{1,0:T(8,128)} %shard_map.82) | data formatting | bytes 524288

commit v2 on v1

--- a/solution.py
+++ b/solution.py
@@ -9,13 +9,13 @@
 from jax.sharding import PartitionSpec as P
 
 TILE = 128
-CHUNKS = 2
+CHUNKS = 4
 MESH = pl.DeviceIdType.MESH
 
 
 class Gather:
     def __init__(self, place, buf, rows, sems):
-        chunks = min(CHUNKS, rows)
+        chunks = math.gcd(CHUNKS, rows)
         self.place, self.buf, self.chunks = place, buf, chunks
         self.step = rows // chunks
         self.rows = rows
@@ -32,7 +32,7 @@
     def carried(self, way, hop):
         if hop < self.place.hops:
             return range(self.chunks)
-        return [way] if way < self.chunks else []
+        return [chunk for chunk in range(self.chunks) if chunk * 2 // self.chunks == way]
 
     def ring_copy(self, way, hop, chunk, scen):
         at = self.slot(way, hop, chunk)
@@ -62,11 +62,18 @@
         copy.start()
         self.sent.append(copy)
 
-    def begin(self):
+    def begin(self, staggered=False):
+        pending = []
         for chunk in range(self.chunks):
+            if staggered:
+                for copy in pending:
+                    copy.wait_send()
+                self.sent = [copy for copy in self.sent if all(copy is not p for p in pending)]
+                pending = []
             for way in range(2):
                 if chunk in self.carried(way, 1):
-                    self.send(self.ring_copy(way, 1, chunk, self.place.scen))
+                    pending.append(self.ring_copy(way, 1, chunk, self.place.scen))
+                    self.send(pending[-1])
         for chunk in range(self.chunks):
             self.send(self.pair_copy(0, 0, chunk, self.place.scen, self.place.core))
 
@@ -189,7 +196,7 @@
     tiles = Gather(place, tiles_all, 1, ring_sems[12:16])
 
     crossings = []
-    low.begin()
+    low.begin(staggered=True)
     for index, (source, target) in enumerate(((border_hbm, border), (inverse_hbm, inverse))):
         crossing = pltpu.make_async_remote_copy(
             src_ref=source.at[0],
@@ -326,7 +333,7 @@
     unit = math.gcd(own_rows, TILE)
     units = own_rows // unit
     for rows in (units, units, touched, 1):
-        chunks = min(CHUNKS, rows)
+        chunks = math.gcd(CHUNKS, rows)
         ring_sems += [pltpu.SemaphoreType.DMA((2 * (hops + 1) * chunks,))] * 4
     vmem = pl.BlockSpec(memory_space=pltpu.VMEM)
     smem = pl.BlockSpec(memory_space=pltpu.SMEM)

time: 59.2 us -> 62.7 us (1.059)
  Pallas kernels: 55.5 us -> 59 us
    pallas_call x1, Pallas kernels: 55.5 us -> 59 us  [local(): pl.pallas_call(functools.partial(kernel, count), out_shape=jax.ShapeDtype...]
where the time goes in v2:
time: 62.7 us; the launch traced here: 62.5 us
  Pallas kernels  59 us (94%)
  local copies, waits for them, and re-layouts  2.84 us (5%)
  between operations  0.66 us (1%)
    pallas_call x1, Pallas kernels, local(): pl.pallas_call(functools.partial(kernel, count), out_shape=jax.ShapeDtype...  59 us
    unnamed x1, local copies, waits for them, and re-layouts  1.67 us

profile of v2, /device:TPU:0, one launch (start us, length us, event | category | flops | bytes accessed | tf_op | source)
XLA Modules:
  0.0 62.5 jit_solution(3265464520437654960)
XLA Ops:
  0.7 1.2 %pad_bitcast_fusion.tiles_row_ref = s32[1,1,128]{2,1,0:T(1,128)} fusion(s32[1,6]{1,0:T(1,128)} %own_tiles_ref.1), kind=kLoop, calls=%fused_computation | loop fusion | bytes 536 | tf_op jit(solution)/shard_map/broadcast_in_dim | solution.py:330
  1.8 59.0 %shard_map.82 = f32[512,128]{1,0:T(8,128)} custom-call(f32[512,128]{1,0:T(8,128)} %guess_ref.1, f32[512,128]{1,0:T(8,128)} %right_ref.1, f32[1,512]{1,0:T(1,128)} %bitcast.3, bf16[512,8192]{1,0:T(8,128)(2,1)} %precon_hbm.1, bf16[1,256,768]{2,1,0:T(8,128)(2,1)} %border_hbm.1, bf16[1,256,512]{2,1,0:T(8,128)(2,1)} %inverse_hbm.1, s32[1]{0:T(128)S(6)} %copy.10.live_ref, ...), custom_call_target="tpu_custom_call" | custom-call | tf_op jit(solution)/shard_map/pallas_call | solution.py:341
  60.8 1.7 %copy.11 = f32[512,128]{1,0:T(8,128)} copy(f32[512,128]{1,0:T(8,128)} %shard_map.82) | data formatting | bytes 524288
